TPU v7x, 32 devices: a whole 2x2x4 slice. The times are simulated.
32 devices in a mesh: rows: 8 (over y, x, core), feat: 4 (over z).
Axes of the slice: x: 2, y: 2, z: 4, core: 2. Of those that a mesh axis runs over, the one named last changes fastest.
Arguments:
- features: bfloat16 [8192, 2048], P('rows', 'feat'), may hold values from -6 to 6
- grad_out: bfloat16 [8192, 2048], P('rows', 'feat'), may hold values from -6 to 6
- eigvecs: float32 [2048, 2048], P('feat', 'rows'), may hold values from -1 to 1, as said below
- eigvals: float32 [2048], replicated, may hold values from 0.1 to 1, as said below
- whiten: bfloat16 [2048, 2048], P(None, 'feat'), may hold values from -0.125 to 0.125
Outputs:
- grad_in: bfloat16 [8192, 2048], P('rows', 'feat')
Inputs may be any that keep to these rules, and one draw needn't show every extreme that they name: `eigvecs`: the columns are orthonormal. `eigvals`: any two entries differ by at least 0.45 / 2048.
All inputs are finite; a program needn't handle non-finite values.
Results may differ from a plain program's by a relative error of at most 0.0074.
Values may be sent and summed in bfloat16 or wider, within the bound.
A program may use at most 128 MiB of HBM per device.

v0:
```python
import jax
import jax.numpy as jnp
from jax import lax
from jax.sharding import PartitionSpec as P


def divided(lam_row, lam_col, first_col):
    on_diag = (
        jnp.arange(lam_row.shape[0], dtype=jnp.int32)[:, None]
        == (first_col + jnp.arange(lam_col.shape[0], dtype=jnp.int32))[None, :]
    )
    root_row = lam_row ** (-0.5)
    root_col = lam_col ** (-0.5)
    gaps_lam = lam_row[:, None] - lam_col[None, :]
    safe_gap = jnp.where(on_diag, jnp.ones_like(gaps_lam), gaps_lam)
    off_diag = (root_row[:, None] - root_col[None, :]) / safe_gap
    diag_vals = -0.5 * lam_row[:, None] ** (-1.5) + jnp.zeros_like(gaps_lam)
    return jnp.where(on_diag, diag_vals, off_diag)


def local(features, grad_out, eigvecs, eigvals, whiten):
    highest = lax.Precision.HIGHEST
    tok_rows, own_cols = features.shape
    row_count = tok_rows * lax.axis_size("rows")
    contract_rows = (((0,), (0,)), ((), ()))
    contract_last = (((1,), (1,)), ((), ()))
    piece_x = lax.all_gather(features, "feat", axis=1, tiled=True)
    piece_g = lax.all_gather(grad_out, "feat", axis=1, tiled=True)
    left_part = lax.dot_general(
        features, piece_g, contract_rows, preferred_element_type=jnp.float32
    )
    right_part = lax.dot_general(
        grad_out, piece_x, contract_rows, preferred_element_type=jnp.float32
    )
    cross_one = left_part
    cross_two = right_part
    sum_x = jnp.sum(piece_x, axis=0, dtype=jnp.float32)
    sum_g = jnp.sum(piece_g, axis=0, dtype=jnp.float32)
    cross_one, cross_two, sum_x, sum_g = (cross_one, cross_two, sum_x, sum_g)
    cross_one, cross_two, sum_x, sum_g = lax.psum((cross_one, cross_two, sum_x, sum_g), "rows")
    both_cross = cross_one + cross_two
    col_mean = sum_x / row_count
    grad_mean = sum_g / row_count
    offset = lax.axis_index("feat") * own_cols
    mean_part = lax.dynamic_slice_in_dim(col_mean, offset, own_cols)
    grad_part = lax.dynamic_slice_in_dim(grad_mean, offset, own_cols)
    sym_gram = 0.5 * (
        both_cross
        - row_count
        * (mean_part[:, None] * grad_mean[None, :] + grad_part[:, None] * col_mean[None, :])
    )
    basis_cols = lax.all_gather(eigvecs, "feat", axis=0, tiled=True)
    basis_block = lax.all_gather(eigvecs, "rows", axis=1, tiled=True)
    narrow = basis_cols.shape[1]
    inner_prod = jnp.dot(sym_gram, basis_cols, precision=highest)
    partial_value = lax.dot_general(basis_block, inner_prod, contract_rows, precision=highest)
    rotated = lax.psum(partial_value, "feat")
    first_col = lax.axis_index("rows") * narrow
    lam_col = lax.dynamic_slice_in_dim(eigvals, first_col, narrow)
    scaled = divided(eigvals, lam_col, first_col) * rotated
    back_rot = jnp.dot(basis_block, scaled, precision=highest)
    sens_own = lax.psum_scatter(
        lax.dot_general(back_rot, basis_cols, contract_last, precision=highest),
        "rows",
        scatter_dimension=0,
        tiled=True,
    )
    scaled_own = (2.0 / row_count * sens_own).astype(jnp.bfloat16)
    sens_scaled = lax.all_gather(scaled_own, "rows", axis=0, tiled=True)
    piece_x = lax.all_gather(features, "feat", axis=1, tiled=True)
    piece_g = lax.all_gather(grad_out, "feat", axis=1, tiled=True)
    shifted = (piece_g.astype(jnp.float32) - grad_mean).astype(jnp.bfloat16)
    centered = (piece_x.astype(jnp.float32) - col_mean).astype(jnp.bfloat16)
    running = jnp.dot(shifted, whiten, preferred_element_type=jnp.float32)
    grad_in = running + lax.dot_general(
        centered, sens_scaled, contract_last, preferred_element_type=jnp.float32
    )
    return grad_in.astype(jnp.bfloat16)


def solution(mesh):
    in_specs = (P("rows", "feat"), P("rows", "feat"), P("feat", "rows"), P(), P(None, "feat"))
    out_specs = P("rows", "feat")
    return jax.shard_map(local, mesh=mesh, in_specs=in_specs, out_specs=out_specs, check_vma=False)
```

profile of v0, /device:TPU:0, one launch (start us, length us, event | category | flops | bytes accessed | tf_op | source)
XLA Modules:
  0.0 552.3 jit_solution(13871746332786428748)
XLA Ops:
  6.5 0.0 copy-start
  6.5 0.0 all-gather.6.cloned.1.call-start
  6.5 0.7 all-gather.6.cloned.1.call-update
  7.3 0.0 all-gather.8.cloned.1.call-start
  7.3 0.7 all-gather.8.cloned.1.call-update
  8.0 0.0 all-gather.10.cloned.1.call-start
  8.1 0.7 all-gather.10.cloned.1.call-update
  8.7 0.0 copy-start.3
  8.8 0.0 all-reduce.6.cloned.1.call-start
  8.8 83.6 %all-gather.6.cloned.1.call-done = bf16[1024,2048]{1,0:T(8,128)(2,1)} async-done(((bf16[1024,512]{1,0:T(8,128)(2,1)}), bf16[1024,2048]{1,0:T(8,128)(2,1)}) %all-gather.6.cloned.1.call-update) | async-done | bytes 4194320 | tf_op jit(solution)/shard_map/all_gather | solution.py:71
  92.4 6.8 %fusion.40 = f32[512,2048]{1,0:T(8,128)} fusion(bf16[1024,512]{1,0:T(8,128)(2,1)} %param.5, bf16[1024,2048]{1,0:T(8,128)(2,1)} %all-gather.6.cloned.1.call-done), kind=kOutput, calls=%fused_computation.51 | convolution fusion | flops 2147483648 | bytes 9437184 | tf_op jit(solution)/shard_map/dot_general | solution.py:29
  99.2 74.0 %all-gather.8.cloned.1.call-done = bf16[1024,2048]{1,0:T(8,128)(2,1)} async-done(((bf16[1024,512]{1,0:T(8,128)(2,1)}), bf16[1024,2048]{1,0:T(8,128)(2,1)}) %all-gather.8.cloned.1.call-update) | async-done | bytes 4194320 | tf_op jit(solution)/shard_map/all_gather | solution.py:70
  173.2 0.0 copy-done.3
  173.2 7.8 %convolution_add_fusion = f32[512,2048]{1,0:T(8,128)} fusion(f32[512,2048]{1,0:T(8,128)} %fusion.40, bf16[1024,512]{1,0:T(8,128)(2,1)S(1)} %copy-done.3, bf16[1024,2048]{1,0:T(8,128)(2,1)} %all-gather.8.cloned.1.call-done), kind=kOutput, calls=%fused_computation.17 | convolution fusion | flops 2148532224 | bytes 13631488 | tf_op jit(solution)/shard_map/dot_general | solution.py:32
  181.0 0.0 all-reduce.6.cloned.1.call-update
  181.1 0.0 all-gather.12.cloned.1.call-start
  181.1 0.5 all-gather.12.cloned.1.call-update
  181.7 0.0 all-reduce.4.cloned.1.call-start
  181.7 0.0 copy-start.1
  181.7 3.0 convert_reduce_fusion
  184.7 0.5 copy-done.1
  185.2 0.6 convert_reduce_fusion.1
  185.8 25.6 %all-reduce = (f32[2048]{0:T(1024)S(1)}, f32[2048]{0:T(1024)S(1)}) all-reduce(f32[2048]{0:T(1024)S(1)} %convert_reduce_fusion, f32[2048]{0:T(1024)S(1)} %convert_reduce_fusion.1), channel_id=1, replica_groups=mesh['rows'=8,'feat'=4] {'rows'}, use_global_device_ids=true, to_apply=%region_3.0 | all-reduce | flops 4096 | bytes 32768 | tf_op jit(solution)/shard_map/psum | solution.py:40
  211.4 0.1 dynamic_slice.10
  211.5 0.1 dynamic_slice.11
  211.6 7.4 %all-gather.10.cloned.1.call-done = f32[2048,256]{1,0:T(8,128)} async-done(((f32[512,256]{1,0:T(8,128)}), f32[2048,256]{1,0:T(8,128)}) %all-gather.10.cloned.1.call-update) | async-done | bytes 2097168 | tf_op jit(solution)/shard_map/all_gather | solution.py:52
  219.0 82.8 %all-reduce.6.cloned.1.call-done = f32[512,2048]{1,0:T(8,128)} async-done(((f32[512,2048]{1,0:T(8,128)}), f32[512,2048]{1,0:T(8,128)}) %all-reduce.6.cloned.1.call-update) | async-done | bytes 4194320 | tf_op jit(solution)/shard_map/psum | solution.py:40
  301.7 6.9 %fusion.6 = f32[512,256]{1,0:T(8,128)S(1)} fusion(f32[2048,256]{1,0:T(8,128)} %all-gather.10.cloned.1.call-done, f32[512,2048]{1,0:T(8,128)} %all-reduce.6.cloned.1.call-done, f32[2048]{0:T(1024)S(1)} %get-tuple-element.11, f32[512]{0:T(512)S(1)} %dynamic_slice.11, f32[2048]{0:T(1024)S(1)} %get-tuple-element.12, f32[512]{0:T(512)S(1)} %dynamic_slice.10), kind=kOutput, calls=%fused_computation.8 | convolution fusion | flops 3227516928 | bytes 6836224 | tf_op jit(solution)/shard_map/dot_general | solution.py:55
  308.6 0.0 copy-start.5
  308.6 32.3 %all-gather.12.cloned.1.call-done = f32[512,2048]{1,0:T(8,128)} async-done(((f32[512,256]{1,0:T(8,128)}), f32[512,2048]{1,0:T(8,128)}) %all-gather.12.cloned.1.call-update) | async-done | bytes 4194320 | tf_op jit(solution)/shard_map/all_gather | solution.py:53
  340.9 10.2 %convolution_bitcast_fusion = f32[2048,256]{1,0:T(8,128)} fusion(f32[512,256]{1,0:T(8,128)S(1)} %fusion.6, f32[512,2048]{1,0:T(8,128)} %all-gather.12.cloned.1.call-done), kind=kOutput, calls=%fused_computation.18 | convolution fusion | flops 3221225472 | bytes 6815744 | tf_op jit(solution)/shard_map/dot_general | solution.py:56
  351.1 0.0 all-reduce.4.cloned.1.call-update
  351.1 0.3 reduce-scatter.2.cloned.1.call-start
  351.4 0.0 copy-done.5
  351.4 0.1 broadcast_power_fusion.1
  351.5 85.9 %all-reduce.4.cloned.1.call-done = f32[2048,256]{1,0:T(8,128)} async-done(((f32[2048,256]{1,0:T(8,128)}), f32[2048,256]{1,0:T(8,128)}) %all-reduce.4.cloned.1.call-update) | async-done | bytes 2097168 | tf_op jit(solution)/shard_map/psum | solution.py:57
  437.4 10.8 %fusion.15 = f32[256,512]{1,0:T(8,128)S(1)} fusion(f32[512,2048]{1,0:T(8,128)} %all-gather.12.cloned.1.call-done, f32[2048,256]{1,0:T(8,128)} %all-reduce.4.cloned.1.call-done, f32[256]{0:T(256)S(1)} %get-tuple-element.8, f32[2048]{0:T(1024)S(1)} %copy-done.5, f32[256]{0:T(256)S(1)} %get-tuple-element.7, f32[2048]{0:T(1024)S(1)} %get-tuple-element.10, ...), kind=kOutput, calls=%fused_computation.20 | convolution fusion | flops 3224895488 | bytes 6843392 | tf_op jit(solution)/shard_map/dot_general | solution.py:61
  448.2 0.0 copy-done.4
  448.2 8.4 %fusion.41 = f32[512,2048]{1,0:T(8,128)} fusion(f32[256,512]{1,0:T(8,128)S(1)} %fusion.15, f32[2048,256]{1,0:T(8,128)S(1)} %copy-done.4), kind=kOutput, calls=%fused_computation.52 | convolution fusion | flops 3221225472 | bytes 6815744 | tf_op jit(solution)/shard_map/dot_general | solution.py:63
  456.6 0.0 reduce-scatter.2.cloned.1.call-update
  456.7 0.3 all-gather.14.cloned.1.call-start
  457.0 50.0 %reduce-scatter.2.cloned.1.call-done = f32[64,2048]{1,0:T(8,128)} async-done(((f32[512,2048]{1,0:T(8,128)}), f32[64,2048]{1,0:T(8,128)}) %reduce-scatter.2.cloned.1.call-update) | async-done | bytes 524304 | tf_op jit(solution)/shard_map/reduce_scatter | solution.py:62
  507.0 1.8 multiply_convert_fusion
  508.8 0.0 all-gather.14.cloned.1.call-update
  508.8 27.9 %all-gather.14.cloned.1.call-done = bf16[512,2048]{1,0:T(8,128)(2,1)} async-done(((bf16[64,2048]{1,0:T(8,128)(2,1)}), bf16[512,2048]{1,0:T(8,128)(2,1)}) %all-gather.14.cloned.1.call-update) | async-done | bytes 2097168 | tf_op jit(solution)/shard_map/all_gather | solution.py:69
  536.7 5.4 fusion.2
  542.1 0.0 copy-done
  542.1 3.3 add_convert_fusion
  (6 shorter events, 0.0 us)
Async XLA Ops:
  6.5 535.6 %copy-start = (bf16[2048,512]{1,0:T(8,128)(2,1)S(1)}, bf16[2048,512]{1,0:T(8,128)(2,1)}, u32[]{:S(2)}) copy-start(bf16[2048,512]{1,0:T(8,128)(2,1)} %param.9) | copy-start | bytes 6291460
  6.5 85.9 %all-gather.6.cloned.1.call-start = ((), (), s32[]{:S(2)}) async-start(), calls=%async_computation.1 | async-start | bytes 5242880 | tf_op jit(solution)/shard_map/all_gather | solution.py:71
  7.3 166.0 %all-gather.8.cloned.1.call-start = ((), (), s32[]{:S(2)}) async-start(), calls=%async_computation.2 | async-start | bytes 5242880 | tf_op jit(solution)/shard_map/all_gather | solution.py:70
  8.0 211.0 %all-gather.10.cloned.1.call-start = ((), (), s32[]{:S(2)}) async-start(), calls=%async_computation.3 | async-start | bytes 2621440 | tf_op jit(solution)/shard_map/all_gather | solution.py:52
  8.7 164.5 %copy-start.3 = (bf16[1024,512]{1,0:T(8,128)(2,1)S(1)}, bf16[1024,512]{1,0:T(8,128)(2,1)}, u32[]{:S(2)}) copy-start(bf16[1024,512]{1,0:T(8,128)(2,1)} %param.6) | copy-start | bytes 3145732
  8.8 293.0 %all-reduce.6.cloned.1.call-start = ((), (), s32[]{:S(2)}) async-start(), calls=%async_computation.8 | async-start | bytes 8388608 | tf_op jit(solution)/shard_map/psum | solution.py:40
  181.1 159.9 %all-gather.12.cloned.1.call-start = ((), (), s32[]{:S(2)}) async-start(), calls=%async_computation.4 | async-start | bytes 4718592 | tf_op jit(solution)/shard_map/all_gather | solution.py:53
  181.7 255.8 %all-reduce.4.cloned.1.call-start = ((), (), s32[]{:S(2)}) async-start(), calls=%async_computation.5 | async-start | bytes 4194304 | tf_op jit(solution)/shard_map/psum | solution.py:57
  181.7 3.5 copy-start.1
  308.6 42.8 %copy-start.5 = (f32[2048]{0:T(1024)S(1)}, f32[2048]{0:T(1024)}, u32[]{:S(2)}) copy-start(f32[2048]{0:T(1024)} %param.8) | copy-start | bytes 24580
  351.1 155.9 %reduce-scatter.2.cloned.1.call-start = ((), (), s32[]{:S(2)}) async-start(), calls=%async_computation.6 | async-start | bytes 4718592 | tf_op jit(solution)/shard_map/reduce_scatter | solution.py:62
  437.4 10.8 %copy-start.4 = (f32[2048,256]{1,0:T(8,128)S(1)}, f32[2048,256]{1,0:T(8,128)}, u32[]{:S(2)}) copy-start(f32[2048,256]{1,0:T(8,128)} %all-gather.10.cloned.1.call-done) | copy-start | bytes 6291460
  456.7 80.1 %all-gather.14.cloned.1.call-start = ((), (), s32[]{:S(2)}) async-start(), calls=%async_computation.7 | async-start | bytes 2359296 | tf_op jit(solution)/shard_map/all_gather | solution.py:69
  536.7 5.4 copy-start.2
Sparse Core Ops, SparseCore 0:
  8.9 83.4 all-gather.5
  94.0 79.2 all-gather.7
  174.8 44.1 all-gather.9
  222.1 79.5 all-reduce.5
  303.5 37.3 all-gather.11
  351.3 86.1 all-reduce.3
  456.8 50.1 reduce-scatter.1
  508.9 27.7 all-gather.13
where the time goes:
time: 552 us
  waiting for transfers between devices  447 us (81%)
  matrix products  59.6 us (11%)
  blocking collectives  25.6 us (5%)
  between operations  13.6 us (2%)
    psum x1, waiting for transfers between devices, local(): rotated = lax.psum(partial_value, 'feat')  85.9 us
    all_gather x1, waiting for transfers between devices, local(): piece_g = lax.all_gather(grad_out, 'feat', axis=1, tiled=True)  83.6 us
    psum x1, waiting for transfers between devices, local(): lax.psum((cross_one, cross_two, sum_x, sum_g), 'rows')  82.8 us
    all_gather x1, waiting for transfers between devices, local(): piece_x = lax.all_gather(features, 'feat', axis=1, tiled=True)  74 us
    reduce_scatter x1, waiting for transfers between devices, local(): lax.psum_scatter(lax.dot_general(back_rot, basis_cols, contract_last, pre...  50 us
    all_gather x1, waiting for transfers between devices, local(): basis_block = lax.all_gather(eigvecs, 'rows', axis=1, tiled=True)  32.3 us
    all_gather x1, waiting for transfers between devices, local(): sens_scaled = lax.all_gather(scaled_own, 'rows', axis=0, tiled=True)  27.9 us
    psum x1, blocking collectives, local(): lax.psum((cross_one, cross_two, sum_x, sum_g), 'rows')  25.6 us
  transfers between devices with their start and end apart: 8, of which 8 were waited for; matrix products, arithmetic and copies ran while one was open for 5% of the time, Pallas kernels for 0%

commit v1 on v0

--- a/solution.py
+++ b/solution.py
@@ -67,8 +67,11 @@
     )
     scaled_own = (2.0 / row_count * sens_own).astype(jnp.bfloat16)
     sens_scaled = lax.all_gather(scaled_own, "rows", axis=0, tiled=True)
-    piece_x = lax.all_gather(features, "feat", axis=1, tiled=True)
-    piece_g = lax.all_gather(grad_out, "feat", axis=1, tiled=True)
+    piece_x, piece_g = jnp.split(
+        lax.all_gather(jnp.concatenate([features, grad_out], axis=0), "feat", axis=1, tiled=True),
+        [features.shape[0]],
+        axis=0,
+    )
     shifted = (piece_g.astype(jnp.float32) - grad_mean).astype(jnp.bfloat16)
     centered = (piece_x.astype(jnp.float32) - col_mean).astype(jnp.bfloat16)
     running = jnp.dot(shifted, whiten, preferred_element_type=jnp.float32)

time: 552 us -> 700 us (1.27)
  waiting for transfers between devices: 447 us -> 587 us
    all_gather x0 -> x1, waiting for transfers between devices: none -> 149 us  [local(): lax.all_gather(jnp.concatenate([features, grad_out], axis=0), 'feat', axi...]
  transfers between devices with their start and end apart: 8 -> 9, of which waited for: 8 -> 9; matrix products, arithmetic and copies ran while one was open for 5% -> 5% of each run, Pallas kernels for 0% -> 0%
where the time goes in v1:
time: 700 us; the launch traced here: 699 us
  waiting for transfers between devices  587 us (84%)
  matrix products  63.4 us (9%)
  blocking collectives  25.6 us (4%)
  between operations  13.3 us (2%)
  other arithmetic  8.14 us (1%)
    all_gather x1, waiting for transfers between devices, local(): lax.all_gather(jnp.concatenate([features, grad_out], axis=0), 'feat', axi...  149 us
    psum x1, waiting for transfers between devices, local(): rotated = lax.psum(partial_value, 'feat')  85.9 us
    all_gather x1, waiting for transfers between devices, local(): piece_g = lax.all_gather(grad_out, 'feat', axis=1, tiled=True)  83.6 us
    psum x1, waiting for transfers between devices, local(): lax.psum((cross_one, cross_two, sum_x, sum_g), 'rows')  82.8 us
    all_gather x1, waiting for transfers between devices, local(): piece_x = lax.all_gather(features, 'feat', axis=1, tiled=True)  74 us
    reduce_scatter x1, waiting for transfers between devices, local(): lax.psum_scatter(lax.dot_general(back_rot, basis_cols, contract_last, pre...  47.2 us
    all_gather x1, waiting for transfers between devices, local(): basis_block = lax.all_gather(eigvecs, 'rows', axis=1, tiled=True)  32.3 us
    psum x1, blocking collectives, local(): lax.psum((cross_one, cross_two, sum_x, sum_g), 'rows')  25.6 us
  transfers between devices with their start and end apart: 9, of which 9 were waited for; matrix products, arithmetic and copies ran while one was open for 5% of the time, Pallas kernels for 0%

profile of v1, /device:TPU:0, one launch (start us, length us, event | category | flops | bytes accessed | tf_op | source)
XLA Modules:
  0.0 699.4 jit_solution(9084135493678189630)
XLA Ops:
  6.5 0.0 all-gather.9.cloned.1.call-start
  6.5 0.7 all-gather.9.cloned.1.call-update
  7.3 0.0 all-gather.11.cloned.1.call-start
  7.3 0.7 all-gather.11.cloned.1.call-update
  8.0 0.0 all-gather.13.cloned.1.call-start
  8.1 0.7 all-gather.13.cloned.1.call-update
  8.7 0.0 copy-start.3
  8.8 0.0 all-reduce.6.cloned.1.call-start
  8.8 83.6 %all-gather.9.cloned.1.call-done = bf16[1024,2048]{1,0:T(8,128)(2,1)} async-done(((bf16[1024,512]{1,0:T(8,128)(2,1)}), bf16[1024,2048]{1,0:T(8,128)(2,1)}) %all-gather.9.cloned.1.call-update) | async-done | bytes 4194320 | tf_op jit(solution)/shard_map/all_gather | solution.py:28
  92.4 6.8 fusion.36
  99.2 74.0 %all-gather.11.cloned.1.call-done = bf16[1024,2048]{1,0:T(8,128)(2,1)} async-done(((bf16[1024,512]{1,0:T(8,128)(2,1)}), bf16[1024,2048]{1,0:T(8,128)(2,1)}) %all-gather.11.cloned.1.call-update) | async-done | bytes 4194320 | tf_op jit(solution)/shard_map/all_gather | solution.py:27
  173.2 7.8 %convolution_add_fusion = f32[512,2048]{1,0:T(8,128)} fusion(f32[512,2048]{1,0:T(8,128)} %fusion.36, bf16[1024,512]{1,0:T(8,128)(2,1)S(1)} %copy-done.3, bf16[1024,2048]{1,0:T(8,128)(2,1)} %all-gather.11.cloned.1.call-done), kind=kOutput, calls=%fused_computation.17 | convolution fusion | flops 2148532224 | bytes 13631488 | tf_op jit(solution)/shard_map/dot_general | solution.py:32
  181.0 0.0 all-reduce.6.cloned.1.call-update
  181.0 0.0 all-gather.15.cloned.1.call-start
  181.1 0.5 all-gather.15.cloned.1.call-update
  181.6 0.0 all-reduce.4.cloned.1.call-start
  181.7 3.0 convert_reduce_fusion
  184.7 0.5 copy-done.1
  185.2 0.6 convert_reduce_fusion.1
  185.8 25.6 %all-reduce = (f32[2048]{0:T(1024)S(1)}, f32[2048]{0:T(1024)S(1)}) all-reduce(f32[2048]{0:T(1024)S(1)} %convert_reduce_fusion.1, f32[2048]{0:T(1024)S(1)} %convert_reduce_fusion), channel_id=1, replica_groups=mesh['rows'=8,'feat'=4] {'rows'}, use_global_device_ids=true, to_apply=%region_1.0 | all-reduce | flops 4096 | bytes 32768 | tf_op jit(solution)/shard_map/psum | solution.py:40
  211.4 0.1 dynamic_slice.10
  211.5 0.1 dynamic_slice.11
  211.6 7.4 %all-gather.13.cloned.1.call-done = f32[2048,256]{1,0:T(8,128)} async-done(((f32[512,256]{1,0:T(8,128)}), f32[2048,256]{1,0:T(8,128)}) %all-gather.13.cloned.1.call-update) | async-done | bytes 2097168 | tf_op jit(solution)/shard_map/all_gather | solution.py:52
  219.0 82.8 %all-reduce.6.cloned.1.call-done = f32[512,2048]{1,0:T(8,128)} async-done(((f32[512,2048]{1,0:T(8,128)}), f32[512,2048]{1,0:T(8,128)}) %all-reduce.6.cloned.1.call-update) | async-done | bytes 4194320 | tf_op jit(solution)/shard_map/psum | solution.py:40
  301.8 6.9 fusion.4
  308.6 0.0 copy-start.5
  308.6 32.3 %all-gather.15.cloned.1.call-done = f32[512,2048]{1,0:T(8,128)} async-done(((f32[512,256]{1,0:T(8,128)}), f32[512,2048]{1,0:T(8,128)}) %all-gather.15.cloned.1.call-update) | async-done | bytes 4194320 | tf_op jit(solution)/shard_map/all_gather | solution.py:53
  340.9 10.2 %convolution_bitcast_fusion = f32[2048,256]{1,0:T(8,128)} fusion(f32[512,256]{1,0:T(8,128)S(1)} %fusion.4, f32[512,2048]{1,0:T(8,128)} %all-gather.15.cloned.1.call-done), kind=kOutput, calls=%fused_computation.18 | convolution fusion | flops 3221225472 | bytes 6815744 | tf_op jit(solution)/shard_map/dot_general | solution.py:56
  351.1 0.0 all-reduce.4.cloned.1.call-update
  351.1 0.3 reduce-scatter.2.cloned.1.call-start
  351.4 0.1 broadcast_power_fusion.1
  351.5 85.9 %all-reduce.4.cloned.1.call-done = f32[2048,256]{1,0:T(8,128)} async-done(((f32[2048,256]{1,0:T(8,128)}), f32[2048,256]{1,0:T(8,128)}) %all-reduce.4.cloned.1.call-update) | async-done | bytes 2097168 | tf_op jit(solution)/shard_map/psum | solution.py:57
  437.4 10.8 %fusion.13 = f32[256,512]{1,0:T(8,128)S(1)} fusion(f32[512,2048]{1,0:T(8,128)} %all-gather.15.cloned.1.call-done, f32[2048,256]{1,0:T(8,128)} %all-reduce.4.cloned.1.call-done, f32[256]{0:T(256)S(1)} %get-tuple-element.8, f32[2048]{0:T(1024)S(1)} %copy-done.5, f32[256]{0:T(256)S(1)} %get-tuple-element.7, f32[2048]{0:T(1024)S(1)} %get-tuple-element.10, ...), kind=kOutput, calls=%fused_computation.21 | convolution fusion | flops 3224895488 | bytes 6843392 | tf_op jit(solution)/shard_map/dot_general | solution.py:61
  448.2 0.0 copy-start.2
  448.2 8.3 %fusion.37 = f32[512,2048]{1,0:T(8,128)} fusion(f32[256,512]{1,0:T(8,128)S(1)} %fusion.13, f32[2048,256]{1,0:T(8,128)S(1)} %copy-done.4), kind=kOutput, calls=%fused_computation.53 | convolution fusion | flops 3221225472 | bytes 6815744 | tf_op jit(solution)/shard_map/dot_general | solution.py:63
  456.6 0.0 reduce-scatter.2.cloned.1.call-update
  456.6 0.0 all-gather.7.cloned.1.call-start
  456.7 0.0 copy-done.2
  456.7 2.7 pad_maximum_fusion
  459.4 0.0 all-gather.7.cloned.1.call-update
  459.4 0.3 all-gather.17.cloned.1.call-start
  459.7 47.2 %reduce-scatter.2.cloned.1.call-done = f32[64,2048]{1,0:T(8,128)} async-done(((f32[512,2048]{1,0:T(8,128)}), f32[64,2048]{1,0:T(8,128)}) %reduce-scatter.2.cloned.1.call-update) | async-done | bytes 524304 | tf_op jit(solution)/shard_map/reduce_scatter | solution.py:62
  507.0 1.8 multiply_convert_fusion
  508.7 0.0 all-gather.17.cloned.1.call-update
  508.8 149.4 %all-gather.7.cloned.1.call-done = bf16[2048,2048]{1,0:T(8,128)(2,1)} async-done(((bf16[2048,512]{1,0:T(8,128)(2,1)}), bf16[2048,2048]{1,0:T(8,128)(2,1)}) %all-gather.7.cloned.1.call-update) | async-done | bytes 8388624 | tf_op jit(solution)/shard_map/all_gather | solution.py:71
  658.2 5.9 fusion
  664.0 22.0 %all-gather.17.cloned.1.call-done = bf16[512,2048]{1,0:T(8,128)(2,1)} async-done(((bf16[64,2048]{1,0:T(8,128)(2,1)}), bf16[512,2048]{1,0:T(8,128)(2,1)}) %all-gather.17.cloned.1.call-update) | async-done | bytes 2097168 | tf_op jit(solution)/shard_map/all_gather | solution.py:69
  686.1 6.8 add_convert_fusion
  (10 shorter events, 0.0 us)
Async XLA Ops:
  6.5 651.6 %copy-start = (bf16[2048,512]{1,0:T(8,128)(2,1)S(1)}, bf16[2048,512]{1,0:T(8,128)(2,1)}, u32[]{:S(2)}) copy-start(bf16[2048,512]{1,0:T(8,128)(2,1)} %param.9) | copy-start | bytes 6291460
  6.5 85.9 %all-gather.9.cloned.1.call-start = ((), (), s32[]{:S(2)}) async-start(), calls=%async_computation.2 | async-start | bytes 5242880 | tf_op jit(solution)/shard_map/all_gather | solution.py:28
  7.3 166.0 %all-gather.11.cloned.1.call-start = ((), (), s32[]{:S(2)}) async-start(), calls=%async_computation.3 | async-start | bytes 5242880 | tf_op jit(solution)/shard_map/all_gather | solution.py:27
  8.0 211.0 %all-gather.13.cloned.1.call-start = ((), (), s32[]{:S(2)}) async-start(), calls=%async_computation.4 | async-start | bytes 2621440 | tf_op jit(solution)/shard_map/all_gather | solution.py:52
  8.7 164.5 %copy-start.3 = (bf16[1024,512]{1,0:T(8,128)(2,1)S(1)}, bf16[1024,512]{1,0:T(8,128)(2,1)}, u32[]{:S(2)}) copy-start(bf16[1024,512]{1,0:T(8,128)(2,1)} %param.6) | copy-start | bytes 3145732
  8.8 293.0 %all-reduce.6.cloned.1.call-start = ((), (), s32[]{:S(2)}) async-start(), calls=%async_computation.9 | async-start | bytes 8388608 | tf_op jit(solution)/shard_map/psum | solution.py:40
  181.0 159.9 %all-gather.15.cloned.1.call-start = ((), (), s32[]{:S(2)}) async-start(), calls=%async_computation.5 | async-start | bytes 4718592 | tf_op jit(solution)/shard_map/all_gather | solution.py:53
  181.6 255.8 %all-reduce.4.cloned.1.call-start = ((), (), s32[]{:S(2)}) async-start(), calls=%async_computation.6 | async-start | bytes 4194304 | tf_op jit(solution)/shard_map/psum | solution.py:57
  181.7 3.5 copy-start.1
  308.6 42.8 %copy-start.5 = (f32[2048]{0:T(1024)S(1)}, f32[2048]{0:T(1024)}, u32[]{:S(2)}) copy-start(f32[2048]{0:T(1024)} %param.8) | copy-start | bytes 24580
  351.1 155.8 %reduce-scatter.2.cloned.1.call-start = ((), (), s32[]{:S(2)}) async-start(), calls=%async_computation.7 | async-start | bytes 4718592 | tf_op jit(solution)/shard_map/reduce_scatter | solution.py:62
  437.4 10.8 %copy-start.4 = (f32[2048,256]{1,0:T(8,128)S(1)}, f32[2048,256]{1,0:T(8,128)}, u32[]{:S(2)}) copy-start(f32[2048,256]{1,0:T(8,128)} %all-gather.13.cloned.1.call-done) | copy-start | bytes 6291460
  448.2 8.4 %copy-start.2 = (bf16[1024,512]{1,0:T(8,128)(2,1)S(1)}, bf16[1024,512]{1,0:T(8,128)(2,1)}, u32[]{:S(2)}) copy-start(bf16[1024,512]{1,0:T(8,128)(2,1)} %param.5) | copy-start | bytes 3145732
  456.6 201.6 %all-gather.7.cloned.1.call-start = ((), (), s32[]{:S(2)}) async-start(), calls=%async_computation.1 | async-start | bytes 10485760 | tf_op jit(solution)/shard_map/all_gather | solution.py:71
  459.4 226.7 %all-gather.17.cloned.1.call-start = ((), (), s32[]{:S(2)}) async-start(), calls=%async_computation.8 | async-start | bytes 2359296 | tf_op jit(solution)/shard_map/all_gather | solution.py:69
Sparse Core Ops, SparseCore 0:
  8.9 83.4 all-gather.8
  94.0 79.2 all-gather.10
  174.8 44.1 all-gather.12
  222.1 79.5 all-reduce.5
  303.5 37.3 all-gather.14
  351.3 86.1 all-reduce.3
  456.7 50.1 reduce-scatter.1
  508.5 149.6 all-gather.6
  660.1 25.9 all-gather.16
